TPU v7x, 32 devices: a whole 2x2x4 slice. The times are simulated.
32 devices in a mesh: rows: 16 (over z, y, x), cols: 2 (over core).
Axes of the slice: x: 2, y: 2, z: 4, core: 2. Of those that a mesh axis runs over, the one named last changes fastest.
Arguments:
- eigvecs: float32 [4096, 2048], P('rows', 'cols'), may hold values from -6 to 6
- reflectors: float32 [32, 4096], P('cols', 'rows'), may hold values from -17 to 17
- starts: int32 [32], replicated, may hold values from 0 to 63
Outputs:
- rotated: float32 [4096, 2048], P('rows', 'cols')
Inputs may be any that keep to these rules, and one draw needn't show every extreme that they name: Sweep j's windows begin at rows starts[j] + k * 64.
All inputs are finite; a program needn't handle non-finite values.
Results may differ from a plain program's by a relative error of at most 0.00011.
Values sent between devices are 32-bit elements; how exact they have to be, the bound alone decides.
A program may use at most 64 MiB of HBM per device.

v0:
```python
import jax
import jax.numpy as jnp
from jax import lax
from jax.sharding import PartitionSpec as P

BAND = 64
SWEEPS = 32


def column_sweep(turned, reflector, offset):
    width = turned.shape[0]
    total_rows = turned.shape[1]
    blocks = total_rows // BAND
    rolled = jnp.roll(turned, -offset, axis=1).reshape(width, blocks, BAND)
    rolled_v = jnp.roll(reflector, -offset).reshape(blocks, BAND)
    squares = jnp.sum(rolled_v * rolled_v, axis=1)
    window = jnp.arange(blocks, dtype=jnp.int32)
    usable = (window + 1) * BAND + offset <= total_rows
    scaled = jnp.where(usable, 2.0 / jnp.where(usable, squares, 1.0), 0.0)
    products = jnp.sum(rolled * rolled_v[None, :, :], axis=2)
    rolled = rolled - (products * scaled[None, :])[:, :, None] * rolled_v[None, :, :]
    return jnp.roll(rolled.reshape(width, total_rows), offset, axis=1)


def per_device(eigvecs, reflectors, starts):
    every_sweep = lax.all_gather(reflectors, "cols", axis=0, tiled=True)
    turned = lax.all_to_all(eigvecs, "rows", split_axis=1, concat_axis=0, tiled=True)
    whole_v = lax.all_gather(every_sweep, "rows", axis=1, tiled=True)
    crossed = turned.T

    def advance(sweep_idx, state):
        return column_sweep(state, whole_v[sweep_idx], starts[sweep_idx])

    crossed = lax.fori_loop(0, SWEEPS, advance, crossed)
    return lax.all_to_all(crossed.T, "rows", split_axis=0, concat_axis=1, tiled=True)


def solution(mesh):
    in_specs = (P("rows", "cols"), P("cols", "rows"), P())
    out_specs = P("rows", "cols")
    return jax.shard_map(
        per_device, mesh=mesh, in_specs=in_specs, out_specs=out_specs, check_vma=False
    )
```

profile of v0, /device:TPU:0, one launch (start us, length us, event | category | flops | bytes accessed | tf_op | source)
XLA Modules:
  0.0 527.9 jit_solution(18121734052208252811)
XLA Ops:
  0.0 2.5 copy.12
  2.5 8.5 %all-to-all-start = ((f32[256,16,64]{0,2,1:T(8,128)}), f32[256,16,64]{0,2,1:T(8,128)S(1)}, u32[]{:S(2)}, u32[]{:S(2)}) async-start(f32[256,16,64]{0,2,1:T(8,128)} %bitcast.2), calls=%async_computation | async-start | bytes 2097152 | tf_op jit(solution)/shard_map/all_to_all | solution.py:27
  12.9 55.0 %all_gather.7 = f32[32,4096]{1,0:T(8,128)} all-gather(f32[32,256]{1,0:T(8,128)S(1)} %all_gather.6), channel_id=1, replica_groups=mesh['rows'=16,'cols'=2] {'rows'}, dimensions={1}, use_global_device_ids=true | all-gather | bytes 557056 | tf_op jit(solution)/shard_map/all_gather | solution.py:28
  68.0 435.8 %while.15 = (s32[]{:T(128)}, f32[64,4096]{1,0:T(8,128)S(1)}, s32[32]{0:T(128)S(1)}, f32[32,4096]{1,0:T(8,128)}, s32[]{:T(128)}, /*index=5*/s32[]{:T(128)}, s32[]{:T(128)}, s32[]{:T(128)}, s32[]{:T(128)}) while((s32[]{:T(128)}, f32[64,4096]{1,0:T(8,128)S(1)}, s32[32]{0:T(128)S(1)}, f32[32,4096]{1,0:T(8,128)}, s32[]{:T(128)}, ...), condition=%wide.region_3.5_spmd, body=%wide.region_0.4_spmd.sunk | while | flops 1847711 | bytes 13845943 | solution.py:34
  72.5 2.0 reshape.75
  86.1 2.0 reshape.75
  99.7 2.0 reshape.75
  113.3 2.0 reshape.75
  126.9 2.0 reshape.75
  140.6 2.0 reshape.75
  154.2 2.0 reshape.75
  167.8 2.0 reshape.75
  181.4 2.0 reshape.75
  195.0 2.0 reshape.75
  208.7 2.0 reshape.75
  222.3 2.0 reshape.75
  235.9 2.0 reshape.75
  249.5 2.0 reshape.75
  263.1 2.0 reshape.75
  276.8 2.0 reshape.75
  290.4 2.0 reshape.75
  304.0 2.0 reshape.75
  317.6 2.0 reshape.75
  331.2 2.0 reshape.75
  344.9 2.0 reshape.75
  358.5 2.0 reshape.75
  372.1 2.0 reshape.75
  385.7 2.0 reshape.75
  399.3 2.0 reshape.75
  453.8 2.0 reshape.75
  494.7 2.0 reshape.75
  503.9 22.7 %all_to_all.38 = f32[16,256,64]{1,2,0:T(8,128)S(1)} all-to-all(f32[16,256,64]{1,2,0:T(8,128)S(1)} %bitcast.23), channel_id=1, replica_groups=mesh['rows'=16,'cols'=2] {'rows'}, dimensions={0} | all-to-all | bytes 2097152 | tf_op jit(solution)/shard_map/all_to_all | solution.py:35
  (430 shorter events, 309.5 us)
Async XLA Ops:
  0.0 11.0 %copy-start = (f32[16,256]{1,0:T(8,128)S(1)}, f32[16,256]{1,0:T(8,128)}, u32[]{:S(2)}) copy-start(f32[16,256]{1,0:T(8,128)} %param.8) | copy-start | bytes 49156
  2.5 65.4 %copy-start.1 = (s32[32]{0:T(128)S(1)}, s32[32]{0:T(128)}, u32[]{:S(2)}) copy-start(s32[32]{0:T(128)} %param.9) | copy-start | bytes 388
  2.5 65.3 %all-to-all-start = ((f32[256,16,64]{0,2,1:T(8,128)}), f32[256,16,64]{0,2,1:T(8,128)S(1)}, u32[]{:S(2)}, u32[]{:S(2)}) async-start(f32[256,16,64]{0,2,1:T(8,128)} %bitcast.2), calls=%async_computation | async-start | bytes 2097152 | tf_op jit(solution)/shard_map/all_to_all | solution.py:27
where the time goes:
time: 532 us; the launch traced here: 528 us
  local copies, waits for them, and re-layouts  190 us (36%)
  other arithmetic  174 us (33%)
  blocking collectives  79.5 us (15%)
  loops' own time  75.8 us (14%)
  starting transfers between devices  8.47 us (2%)
    another operation x1, loops' own time, per_device(): crossed = lax.fori_loop(0, SWEEPS, advance, crossed)  75.8 us
    mul x64, local copies, waits for them, and re-layouts, column_sweep(): (products * scaled[None, :])[:, :, None] * rolled_v[None, :, :]  71.3 us
    reshape x32, local copies, waits for them, and re-layouts, column_sweep(): rolled = jnp.roll(turned, -offset, axis=1).reshape(width, blocks, BAND)  63.9 us
    sub x32, other arithmetic, column_sweep(): rolled - (products * scaled[None, :])[:, :, None] * rolled_v[None, :, :]  58.7 us
    all_gather x1, blocking collectives, per_device(): whole_v = lax.all_gather(every_sweep, 'rows', axis=1, tiled=True)  55 us
    concatenate x32, other arithmetic, column_sweep(): rolled = jnp.roll(turned, -offset, axis=1).reshape(width, blocks, BAND)  50.8 us
    dynamic_slice x64, local copies, waits for them, and re-layouts, advance(): return column_sweep(state, whole_v[sweep_idx], starts[sweep_idx])  48.1 us
    all_to_all x1, blocking collectives, per_device(): lax.all_to_all(crossed.T, 'rows', split_axis=0, concat_axis=1, tiled=True)  22.7 us
  transfers between devices with their start and end apart: 1, of which 0 were waited for; matrix products, arithmetic and copies ran while one was open for 0% of the time, Pallas kernels for 0%

commit v1 on v0

--- a/solution.py
+++ b/solution.py
@@ -25,7 +25,8 @@
 def per_device(eigvecs, reflectors, starts):
     every_sweep = lax.all_gather(reflectors, "cols", axis=0, tiled=True)
     turned = lax.all_to_all(eigvecs, "rows", split_axis=1, concat_axis=0, tiled=True)
-    whole_v = lax.all_gather(every_sweep, "rows", axis=1, tiled=True)
+    parts = lax.all_gather(every_sweep, "rows", axis=0, tiled=False)
+    whole_v = jnp.concatenate(parts, axis=1)
     crossed = turned.T
 
     def advance(sweep_idx, state):

time: 532 us -> 531 us (level)
  no operation moved by 1% of the time
where the time goes in v1:
time: 531 us; the launch traced here: 527 us
  local copies, waits for them, and re-layouts  191 us (36%)
  other arithmetic  174 us (33%)
  blocking collectives  77.4 us (15%)
  loops' own time  75.8 us (14%)
  starting transfers between devices  8.34 us (2%)
    another operation x1, loops' own time, per_device(): crossed = lax.fori_loop(0, SWEEPS, advance, crossed)  75.8 us
    mul x64, local copies, waits for them, and re-layouts, column_sweep(): (products * scaled[None, :])[:, :, None] * rolled_v[None, :, :]  71.3 us
    reshape x32, local copies, waits for them, and re-layouts, column_sweep(): rolled = jnp.roll(turned, -offset, axis=1).reshape(width, blocks, BAND)  63.9 us
    sub x32, other arithmetic, column_sweep(): rolled - (products * scaled[None, :])[:, :, None] * rolled_v[None, :, :]  58.7 us
    all_gather x1, blocking collectives, per_device(): parts = lax.all_gather(every_sweep, 'rows', axis=0, tiled=False)  52.7 us
    concatenate x32, other arithmetic, column_sweep(): rolled = jnp.roll(turned, -offset, axis=1).reshape(width, blocks, BAND)  50.8 us
    dynamic_slice x64, local copies, waits for them, and re-layouts, advance(): return column_sweep(state, whole_v[sweep_idx], starts[sweep_idx])  48.1 us
    all_to_all x1, blocking collectives, per_device(): lax.all_to_all(crossed.T, 'rows', split_axis=0, concat_axis=1, tiled=True)  22.9 us
  transfers between devices with their start and end apart: 1, of which 0 were waited for; matrix products, arithmetic and copies ran while one was open for 0% of the time, Pallas kernels for 0%

profile of v1, /device:TPU:0, one launch (start us, length us, event | category | flops | bytes accessed | tf_op | source)
XLA Modules:
  0.0 526.5 jit_solution(9435078000530873760)
XLA Ops:
  0.0 2.5 copy.15
  2.5 8.3 %all-to-all-start = ((f32[256,16,64]{0,2,1:T(8,128)}), f32[256,16,64]{0,2,1:T(8,128)S(1)}, u32[]{:S(2)}, u32[]{:S(2)}) async-start(f32[256,16,64]{0,2,1:T(8,128)} %bitcast.2), calls=%async_computation | async-start | bytes 2097152 | tf_op jit(solution)/shard_map/all_to_all | solution.py:27
  12.7 52.7 %all-gather = f32[512,256]{1,0:T(8,128)S(1)} all-gather(f32[32,256]{1,0:T(8,128)S(1)} %all_gather.9), channel_id=2, replica_groups=mesh['rows'=16,'cols'=2] {'rows'}, dimensions={0}, use_global_device_ids=true | all-gather | bytes 557056 | tf_op jit(solution)/shard_map/all_gather | solution.py:28
  66.4 435.8 %while.15 = (s32[]{:T(128)}, f32[64,4096]{1,0:T(8,128)S(1)}, s32[32]{0:T(128)S(1)}, f32[32,4096]{1,0:T(8,128)}, s32[]{:T(128)}, /*index=5*/s32[]{:T(128)}, s32[]{:T(128)}, s32[]{:T(128)}, s32[]{:T(128)}) while((s32[]{:T(128)}, f32[64,4096]{1,0:T(8,128)S(1)}, s32[32]{0:T(128)S(1)}, f32[32,4096]{1,0:T(8,128)}, s32[]{:T(128)}, ...), condition=%wide.region_3.5_spmd, body=%wide.region_0.4_spmd.sunk | while | flops 1847711 | bytes 13845943 | solution.py:35
  70.9 2.0 reshape.84
  84.5 2.0 reshape.84
  98.1 2.0 reshape.84
  111.7 2.0 reshape.84
  125.3 2.0 reshape.84
  138.9 2.0 reshape.84
  152.6 2.0 reshape.84
  166.2 2.0 reshape.84
  179.8 2.0 reshape.84
  193.4 2.0 reshape.84
  207.0 2.0 reshape.84
  220.7 2.0 reshape.84
  234.3 2.0 reshape.84
  247.9 2.0 reshape.84
  261.5 2.0 reshape.84
  275.1 2.0 reshape.84
  288.8 2.0 reshape.84
  302.4 2.0 reshape.84
  316.0 2.0 reshape.84
  329.6 2.0 reshape.84
  343.2 2.0 reshape.84
  356.9 2.0 reshape.84
  370.5 2.0 reshape.84
  384.1 2.0 reshape.84
  397.7 2.0 reshape.84
  411.3 2.0 reshape.84
  425.0 2.0 reshape.84
  502.3 22.9 %all_to_all.38 = f32[16,256,64]{1,2,0:T(8,128)S(1)} all-to-all(f32[16,256,64]{1,2,0:T(8,128)S(1)} %bitcast.29), channel_id=1, replica_groups=mesh['rows'=16,'cols'=2] {'rows'}, dimensions={0} | all-to-all | bytes 2097152 | tf_op jit(solution)/shard_map/all_to_all | solution.py:36
  (431 shorter events, 310.3 us)
Async XLA Ops:
  0.0 10.9 %copy-start = (f32[16,256]{1,0:T(8,128)S(1)}, f32[16,256]{1,0:T(8,128)}, u32[]{:S(2)}) copy-start(f32[16,256]{1,0:T(8,128)} %param.8) | copy-start | bytes 49156
  2.5 63.7 %all-to-all-start = ((f32[256,16,64]{0,2,1:T(8,128)}), f32[256,16,64]{0,2,1:T(8,128)S(1)}, u32[]{:S(2)}, u32[]{:S(2)}) async-start(f32[256,16,64]{0,2,1:T(8,128)} %bitcast.2), calls=%async_computation | async-start | bytes 2097152 | tf_op jit(solution)/shard_map/all_to_all | solution.py:27
  10.9 55.5 %copy-start.1 = (s32[32]{0:T(128)S(1)}, s32[32]{0:T(128)}, u32[]{:S(2)}) copy-start(s32[32]{0:T(128)} %param.9) | copy-start | bytes 388
